TPU v7x, 32 devices: a whole 2x2x4 slice. The times are simulated.
32 devices in a mesh: member: 2 (over x), lat: 16 (over z, y, core).
Axes of the slice: x: 2, y: 2, z: 4, core: 2. Of those that a mesh axis runs over, the one named last changes fastest.
Arguments:
- field: bfloat16 [192, 1440, 256], P(('member', 'lat')), parts along dimension 0, may hold values from -3000 to 3000
- gain: float32 [256], replicated, may hold values from 0.1 to 1.9
- slot_wave: int32 [96], replicated, may hold values from 0 to 96, as said below
- legendre: bfloat16 [96, 96, 96], P('lat'), may hold values from -0.625 to 0.625
- mixing: bfloat16 [96, 2, 256, 256], P('lat'), may hold values from -0.25 to 0.25
Outputs:
- result: bfloat16 [192, 1440, 256], P(('member', 'lat')), parts along dimension 0
There are 2 independent parts, one for each index of `member`. A program takes and returns all parts, laid end to end along the dimension named above; an argument that names none is the same for every part. Nothing has to cross between parts.
Inputs may be any that keep to these rules, and one draw needn't show every extreme that they name: `slot_wave`: each wavenumber 0 to 95 stands in exactly one slot and every other slot holds 96; slots 2k and 2k+1 of one lat index hold wavenumbers adding up to (4k+2)16 - 1 where both are below 96.
All inputs are finite; a program needn't handle non-finite values.
Results may differ from a plain program's by a relative error of at most 0.0085.
Values may be sent and summed in bfloat16 or wider, within the bound.
No kernel may reach another device: no remote copies, remote signals or barrier semaphores. Data moves between devices by JAX's collectives and lax.ppermute only.
A program may use at most 64 MiB of HBM per device.

v0:
```python
import math
import jax
import jax.numpy as jnp
from jax import lax
from jax.sharding import PartitionSpec as P


def phase_tables(waves, width):
    points = jnp.arange(width, dtype=jnp.int32)
    phase = (waves[:, None] * points[None, :] % width).astype(jnp.float32) * (2.0 * math.pi / width)
    return (jnp.cos(phase), jnp.sin(phase))


def block_weight(mixing):
    real_part = mixing[:, 0]
    imag_part = mixing[:, 1]
    upper = jnp.concatenate([real_part, imag_part], axis=2)
    lower = jnp.concatenate([-imag_part, real_part], axis=2)
    return jnp.concatenate([upper, lower], axis=1)


def per_device(field, gain, slot_wave, legendre, mixing):
    lat_count = lax.axis_size("lat")
    lat_dev, width, chans = field.shape
    slot_dev, degs, nlat = legendre.shape
    count = float(lat_dev * lat_count * width)
    values = field.astype(jnp.float32)
    local_sum = jnp.sum(values, axis=(0, 1))
    local_sq = jnp.sum(values * values, axis=(0, 1))
    total, squares = lax.psum((local_sum, local_sq), "lat")
    mean = total / count
    var = squares / count - mean * mean
    normed = ((values - mean) * (gain / jnp.sqrt(var + 1e-05))).astype(jnp.bfloat16)
    cosine, sine = phase_tables(slot_wave, width)
    forward = jnp.stack([cosine, -sine]).astype(jnp.bfloat16).reshape(2, lat_count, slot_dev, width)
    weight_m = jnp.where(slot_wave == 0, 1.0, 2.0).astype(jnp.float32)[:, None]
    inverse = jnp.stack([weight_m * cosine, -weight_m * sine]).astype(jnp.bfloat16)
    inv_root = 1.0 / math.sqrt(width)
    spectrum = (
        jnp.einsum("anc,rdjn->dajrc", normed, forward, preferred_element_type=jnp.float32)
        * inv_root
    )
    spectrum = spectrum.astype(jnp.bfloat16).reshape(lat_count, lat_dev, slot_dev, 2 * chans)
    arrived = lax.all_to_all(spectrum, "lat", split_axis=0, concat_axis=1, tiled=True)[0]
    mine = lax.dynamic_slice_in_dim(slot_wave, lax.axis_index("lat") * slot_dev, slot_dev, 0)
    big = block_weight(mixing)
    lat_scale = math.sqrt(nlat / degs)
    degrees = jnp.arange(degs, dtype=jnp.int32)
    coef = jnp.einsum("jlt,tjc->jlc", legendre, arrived, preferred_element_type=jnp.float32)
    coef = jnp.where((degrees[None, :] >= mine[:, None])[:, :, None], coef, 0.0).astype(
        jnp.bfloat16
    )
    mixed = jnp.einsum("jlc,jcd->jld", coef, big, preferred_element_type=jnp.float32).astype(
        jnp.bfloat16
    )
    back = (
        jnp.einsum("jlt,jld->tjd", legendre, mixed, preferred_element_type=jnp.float32) * lat_scale
    )
    back = back.astype(jnp.bfloat16)
    back = back.reshape(lat_count, lat_dev, slot_dev, 2 * chans)
    returned = lax.all_to_all(back, "lat", split_axis=0, concat_axis=2, tiled=True)[0]
    returned = returned.reshape(lat_dev, slot_dev * lat_count, 2, chans)
    filtered = (
        jnp.einsum("akrc,rkn->anc", returned, inverse, preferred_element_type=jnp.float32)
        * inv_root
    )
    return (normed.astype(jnp.float32) + filtered).astype(jnp.bfloat16)


def solution(mesh):
    return jax.shard_map(
        per_device,
        mesh=mesh,
        in_specs=(
            P(("member", "lat"), None, None),
            P(),
            P(),
            P("lat", None, None),
            P("lat", None, None, None),
        ),
        out_specs=P(("member", "lat"), None, None),
        check_vma=False,
    )
```

profile of v0, /device:TPU:9, one launch (start us, length us, event | category | flops | bytes accessed | tf_op | source)
XLA Modules:
  0.0 103.9 jit_solution(11740767256744801090)
XLA Ops:
  0.0 0.0 copy-start
  0.0 0.0 copy-start.2
  0.0 0.0 copy-start.3
  0.0 3.5 %convert_reduce_fusion = (f32[256]{0:T(256)S(1)}, f32[256]{0:T(256)S(1)}) fusion(bf16[6,1440,256]{2,1,0:T(8,128)(2,1)} %param.5), kind=kLoop, calls=%fused_computation.2 | loop fusion | flops 8846848 | bytes 4425728 | tf_op jit(solution)/shard_map/reduce_sum | solution.py:28
  3.5 0.0 copy-done.2
  3.5 0.1 mul.154
  3.6 0.1 copy.23
  3.7 2.8 %cosine_convert_fusion = (bf16[1,16,6,1440]{3,1,2,0:T(8,128)(2,1)S(1)}, bf16[1,16,6,1440]{3,1,2,0:T(8,128)(2,1)S(1)}) fusion(s32[16,6]{0,1:T(8,128)S(1)} %copy.23), kind=kLoop, calls=%fused_computation.44 | loop fusion | flops 1658880 | bytes 553344 | tf_op jit(solution)/shard_map/convert
  6.5 22.3 %all-reduce = (f32[256]{0:T(256)S(1)}, f32[256]{0:T(256)S(1)}) all-reduce(f32[256]{0:T(256)S(1)} %get-tuple-element.6, f32[256]{0:T(256)S(1)} %get-tuple-element.5), channel_id=1, replica_groups=mesh['member'=2,'lat'=16] {'lat'}, use_global_device_ids=true, to_apply=%region_3.0 | all-reduce | flops 512 | bytes 4096 | tf_op jit(solution)/shard_map/psum | solution.py:30
  28.8 0.0 copy-done.3
  28.9 3.6 %fusion.26 = bf16[16,6,6,2,256]{4,0,1,2,3:T(8,128)(2,1)S(1)} fusion(f32[256]{0:T(256)S(1)} %get-tuple-element.14, f32[256]{0:T(256)S(1)} %get-tuple-element.13, bf16[6,1440,256]{2,1,0:T(8,128)(2,1)} %param.5, bf16[1,16,6,1440]{3,1,2,0:T(8,128)(2,1)S(1)} %get-tuple-element.12, bf16[1,16,6,1440]{3,1,2,0:T(8,128)(2,1)S(1)} %get-tuple-element.11), kind=kOutput, calls=%fused_computation.26 | convolution fusion | flops 859889664 | bytes 5568512 | tf_op jit(solution)/shard_map/anc,rdjn->dajrc/dot_general | solution.py:40
  32.5 0.0 copy-start.1
  32.5 0.6 copy.37
  33.1 1.3 %reshape.223 = bf16[16,6,6,512]{3,2,1,0:T(8,128)(2,1)} reshape(bf16[16,6,6,2,256]{4,3,2,1,0:T(2,128)(2,1)S(1)} %copy.37) | data formatting | bytes 1179648 | tf_op jit(solution)/shard_map/reshape | solution.py:43
  34.4 15.3 %all-to-all-start = ((bf16[16,6,6,512]{3,2,1,0:T(8,128)(2,1)}), bf16[16,6,6,512]{3,2,1,0:T(8,128)(2,1)S(1)}, u32[]{:S(2)}, u32[]{:S(2)}) async-start(bf16[16,6,6,512]{3,2,1,0:T(8,128)(2,1)} %reshape.223), calls=%async_computation | async-start | bytes 1572864 | tf_op jit(solution)/shard_map/all_to_all | solution.py:44
  49.7 0.1 dynamic_slice.3
  49.8 0.1 iota_compare_fusion
  49.9 0.0 copy-done.1
  49.9 0.1 fusion.52
  49.9 1.3 %slice_bitcast_fusion = (bf16[6,256,256]{2,1,0:T(8,128)(2,1)}, bf16[6,256,256]{2,1,0:T(8,128)(2,1)}) fusion(bf16[6,2,256,256]{3,2,1,0:T(8,128)(2,1)S(1)} %copy-done.1), kind=kLoop, calls=%fused_computation.29 | loop fusion | bytes 3145728 | tf_op jit(solution)/shard_map/squeeze | solution.py:16
  51.2 18.2 %all-to-all-done = bf16[16,6,6,512]{3,2,1,0:T(8,128)(2,1)S(1)} async-done(((bf16[16,6,6,512]{3,2,1,0:T(8,128)(2,1)}), bf16[16,6,6,512]{3,2,1,0:T(8,128)(2,1)S(1)}, u32[]{:S(2)}, u32[]{:S(2)}) %all-to-all-start) | async-done | bytes 589856 | tf_op jit(solution)/shard_map/all_to_all | solution.py:44
  69.4 0.0 copy-done
  69.4 0.4 fusion.18
  69.7 2.4 %fusion.25 = bf16[96,6,512]{2,0,1:T(8,128)(2,1)S(1)} fusion(bf16[6,96,96]{2,1,0:T(8,128)(2,1)S(1)} %copy-done, bf16[6,512,96]{1,2,0:T(8,128)(2,1)S(1)} %fusion.18, bf16[6,256,256]{2,1,0:T(8,128)(2,1)} %get-tuple-element.10, bf16[6,256,256]{2,1,0:T(8,128)(2,1)S(1)} %fusion.52, bf16[6,256,256]{2,1,0:T(8,128)(2,1)} %get-tuple-element.9), kind=kOutput, calls=%fused_computation.25 | convolution fusion | flops 371785728 | bytes 3649536 | tf_op jit(solution)/shard_map/jlt,jld->tjd/dot_general | solution.py:57
  72.2 0.2 reshape.218
  72.4 1.0 copy.30
  73.3 4.4 %all-to-all-start.1 = ((bf16[16,6,6,512]{3,1,2,0:T(8,128)(2,1)}), bf16[16,6,6,512]{3,1,2,0:T(8,128)(2,1)S(1)}, u32[]{:S(2)}, u32[]{:S(2)}) async-start(bf16[16,6,6,512]{3,1,2,0:T(8,128)(2,1)} %copy.30), calls=%async_computation.1 | async-start | bytes 1572864 | tf_op jit(solution)/shard_map/all_to_all | solution.py:61
  77.8 2.9 %multiply_convert_fusion.1 = (bf16[1,96,1440]{2,1,0:T(8,128)(2,1)S(1)}, bf16[1,96,1440]{2,1,0:T(8,128)(2,1)S(1)}) fusion(s32[96]{0:T(128)S(1)} %copy-done.2, f32[96]{0:T(128)S(1)} %get-tuple-element.17, f32[96]{0:T(128)S(1)} %get-tuple-element.18), kind=kLoop, calls=%fused_computation.49 | loop fusion | flops 1797120 | bytes 554112 | tf_op jit(solution)/shard_map/convert.2
  80.6 16.7 %all-to-all-done.1 = bf16[16,6,6,512]{3,1,2,0:T(8,128)(2,1)S(1)} async-done(((bf16[16,6,6,512]{3,1,2,0:T(8,128)(2,1)}), bf16[16,6,6,512]{3,1,2,0:T(8,128)(2,1)S(1)}, u32[]{:S(2)}, u32[]{:S(2)}) %all-to-all-start.1) | async-done | bytes 589856 | tf_op jit(solution)/shard_map/all_to_all | solution.py:61
  97.4 0.3 reshape.224
  97.7 6.2 %fusion.3 = bf16[6,1440,256]{2,1,0:T(8,128)(2,1)} fusion(f32[256]{0:T(256)S(1)} %get-tuple-element.14, f32[256]{0:T(256)S(1)} %get-tuple-element.13, bf16[6,1440,256]{2,1,0:T(8,128)(2,1)} %param.5, bf16[1,96,1440]{2,1,0:T(8,128)(2,1)S(1)} %get-tuple-element.16, bf16[1,96,1440]{2,1,0:T(8,128)(2,1)S(1)} %get-tuple-element.15, ...), kind=kOutput, calls=%fused_computation.7 | convolution fusion | flops 868147200 | bytes 9992192 | tf_op jit(solution)/shard_map/akrc,rkn->anc/dot_general | solution.py:64
  (2 shorter events, 0.0 us)
Async XLA Ops:
  0.0 69.4 %copy-start = (bf16[6,96,96]{2,1,0:T(8,128)(2,1)S(1)}, bf16[6,96,96]{2,1,0:T(8,128)(2,1)}, u32[]{:S(2)}) copy-start(bf16[6,96,96]{2,1,0:T(8,128)(2,1)} %param.8) | copy-start | bytes 331780
  0.0 3.5 %copy-start.2 = (s32[96]{0:T(128)S(1)}, s32[96]{0:T(128)}, u32[]{:S(2)}) copy-start(s32[96]{0:T(128)} %param.7) | copy-start | bytes 1156
  0.0 28.8 %copy-start.3 = (f32[256]{0:T(256)S(1)}, f32[256]{0:T(256)}, u32[]{:S(2)}) copy-start(f32[256]{0:T(256)} %param.6) | copy-start | bytes 3076
  32.5 17.4 %copy-start.1 = (bf16[6,2,256,256]{3,2,1,0:T(8,128)(2,1)S(1)}, bf16[6,2,256,256]{3,2,1,0:T(8,128)(2,1)}, u32[]{:S(2)}) copy-start(bf16[6,2,256,256]{3,2,1,0:T(8,128)(2,1)} %param.9) | copy-start | bytes 4718596
  34.4 34.9 %all-to-all-start = ((bf16[16,6,6,512]{3,2,1,0:T(8,128)(2,1)}), bf16[16,6,6,512]{3,2,1,0:T(8,128)(2,1)S(1)}, u32[]{:S(2)}, u32[]{:S(2)}) async-start(bf16[16,6,6,512]{3,2,1,0:T(8,128)(2,1)} %reshape.223), calls=%async_computation | async-start | bytes 1572864 | tf_op jit(solution)/shard_map/all_to_all | solution.py:44
  73.3 24.0 %all-to-all-start.1 = ((bf16[16,6,6,512]{3,1,2,0:T(8,128)(2,1)}), bf16[16,6,6,512]{3,1,2,0:T(8,128)(2,1)S(1)}, u32[]{:S(2)}, u32[]{:S(2)}) async-start(bf16[16,6,6,512]{3,1,2,0:T(8,128)(2,1)} %copy.30), calls=%async_computation.1 | async-start | bytes 1572864 | tf_op jit(solution)/shard_map/all_to_all | solution.py:61
where the time goes:
time: 104 us
  waiting for transfers between devices  34.9 us (34%)
  blocking collectives  22.3 us (21%)
  starting transfers between devices  19.7 us (19%)
  matrix products  12.6 us (12%)
  other arithmetic  9.31 us (9%)
  local copies, waits for them, and re-layouts  4.87 us (5%)
    psum x1, blocking collectives, per_device(): total, squares = lax.psum((local_sum, local_sq), 'lat')  22.3 us
    all_to_all x1, waiting for transfers between devices, per_device(): lax.all_to_all(spectrum, 'lat', split_axis=0, concat_axis=1, tiled=True)[0]  18.2 us
    all_to_all x1, waiting for transfers between devices, per_device(): lax.all_to_all(back, 'lat', split_axis=0, concat_axis=2, tiled=True)[0]  16.7 us
    all_to_all x1, starting transfers between devices, per_device(): lax.all_to_all(spectrum, 'lat', split_axis=0, concat_axis=1, tiled=True)[0]  15.3 us
    dot_general x1, matrix products, per_device(): jnp.einsum('akrc,rkn->anc', returned, inverse, preferred_element_type=jnp...  6.16 us
    another operation x2, other arithmetic  5.69 us
    all_to_all x1, starting transfers between devices, per_device(): lax.all_to_all(back, 'lat', split_axis=0, concat_axis=2, tiled=True)[0]  4.42 us
    dot_general x1, matrix products, per_device(): jnp.einsum('anc,rdjn->dajrc', normed, forward, preferred_element_type=jnp...  3.65 us
  transfers between devices with their start and end apart: 2, of which 2 were waited for; matrix products, arithmetic and copies ran while one was open for 4% of the time, Pallas kernels for 0%

commit v1 on v0

--- a/solution.py
+++ b/solution.py
@@ -41,7 +41,13 @@
         * inv_root
     )
     spectrum = spectrum.astype(jnp.bfloat16).reshape(lat_count, lat_dev, slot_dev, 2 * chans)
-    arrived = lax.all_to_all(spectrum, "lat", split_axis=0, concat_axis=1, tiled=True)[0]
+    _bring_task = lambda device_axis, xx, ndim_at, join_dim: jnp.concatenate(
+        lax.all_to_all(
+            jnp.stack(jnp.split(xx, lax.axis_size(device_axis), join_dim), 0), device_axis, 0, 0
+        ),
+        ndim_at,
+    )
+    arrived = _bring_task("lat", spectrum, 1, 0)[0]
     mine = lax.dynamic_slice_in_dim(slot_wave, lax.axis_index("lat") * slot_dev, slot_dev, 0)
     big = block_weight(mixing)
     lat_scale = math.sqrt(nlat / degs)

time: 104 us -> 115 us (1.11)
  local copies, waits for them, and re-layouts: 4.87 us -> 15 us
    unnamed x8 -> x23, local copies, waits for them, and re-layouts: 0.02 us -> 9.37 us
    reshape x2 -> x0, local copies, waits for them, and re-layouts: 1.88 us -> none  [per_device(): spectrum.astype(jnp.bfloat16)]
    split x0 -> x17, local copies, waits for them, and re-layouts: none -> 1.58 us  [per_device(): jnp.split(xx, lax.axis_size(device_axis), join_dim)]
where the time goes in v1:
time: 115 us; the launch traced here: 114 us
  waiting for transfers between devices  34.9 us (30%)
  blocking collectives  22.3 us (19%)
  starting transfers between devices  19.7 us (17%)
  local copies, waits for them, and re-layouts  15 us (13%)
  matrix products  12.6 us (11%)
  other arithmetic  9.31 us (8%)
    psum x1, blocking collectives, per_device(): total, squares = lax.psum((local_sum, local_sq), 'lat')  22.3 us
    all_to_all x1, waiting for transfers between devices, per_device(): lax.all_to_all(jnp.stack(jnp.split(xx, lax.axis_size(device_axis), join_d...  18.2 us
    all_to_all x1, waiting for transfers between devices, per_device(): lax.all_to_all(back, 'lat', split_axis=0, concat_axis=2, tiled=True)[0]  16.7 us
    all_to_all x1, starting transfers between devices, per_device(): lax.all_to_all(jnp.stack(jnp.split(xx, lax.axis_size(device_axis), join_d...  15.3 us
    unnamed x23, local copies, waits for them, and re-layouts  9.37 us
    dot_general x1, matrix products, per_device(): jnp.einsum('akrc,rkn->anc', returned, inverse, preferred_element_type=jnp...  6.16 us
    another operation x2, other arithmetic  5.69 us
    all_to_all x1, starting transfers between devices, per_device(): lax.all_to_all(back, 'lat', split_axis=0, concat_axis=2, tiled=True)[0]  4.42 us
  transfers between devices with their start and end apart: 2, of which 2 were waited for; matrix products, arithmetic and copies ran while one was open for 4% of the time, Pallas kernels for 0%

profile of v1, /device:TPU:9, one launch (start us, length us, event | category | flops | bytes accessed | tf_op | source)
XLA Modules:
  0.0 114.3 jit_solution(14937252957286129905)
XLA Ops:
  0.0 0.0 copy-start
  0.0 0.0 copy-start.2
  0.0 0.0 copy-start.3
  0.0 3.5 %convert_reduce_fusion = (f32[256]{0:T(256)S(1)}, f32[256]{0:T(256)S(1)}) fusion(bf16[6,1440,256]{2,1,0:T(8,128)(2,1)} %param.5), kind=kLoop, calls=%fused_computation.2 | loop fusion | flops 8846848 | bytes 4425728 | tf_op jit(solution)/shard_map/reduce_sum | solution.py:28
  3.5 0.0 copy-done.2
  3.5 0.1 mul.154
  3.6 0.1 copy.54
  3.7 2.8 %cosine_convert_fusion = (bf16[1,16,6,1440]{3,1,2,0:T(8,128)(2,1)S(1)}, bf16[1,16,6,1440]{3,1,2,0:T(8,128)(2,1)S(1)}) fusion(s32[16,6]{0,1:T(8,128)S(1)} %copy.54), kind=kLoop, calls=%fused_computation.44 | loop fusion | flops 1658880 | bytes 553344 | tf_op jit(solution)/shard_map/convert
  6.5 22.3 %all-reduce = (f32[256]{0:T(256)S(1)}, f32[256]{0:T(256)S(1)}) all-reduce(f32[256]{0:T(256)S(1)} %get-tuple-element.6, f32[256]{0:T(256)S(1)} %get-tuple-element.5), channel_id=1, replica_groups=mesh['member'=2,'lat'=16] {'lat'}, use_global_device_ids=true, to_apply=%region_3.0 | all-reduce | flops 512 | bytes 4096 | tf_op jit(solution)/shard_map/psum | solution.py:30
  28.8 0.0 copy-done.3
  28.9 3.6 %fusion.26 = bf16[16,6,6,2,256]{4,0,1,2,3:T(8,128)(2,1)S(1)} fusion(f32[256]{0:T(256)S(1)} %get-tuple-element.30, f32[256]{0:T(256)S(1)} %get-tuple-element.29, bf16[6,1440,256]{2,1,0:T(8,128)(2,1)} %param.5, bf16[1,16,6,1440]{3,1,2,0:T(8,128)(2,1)S(1)} %get-tuple-element.28, bf16[1,16,6,1440]{3,1,2,0:T(8,128)(2,1)S(1)} %get-tuple-element.27), kind=kOutput, calls=%fused_computation.26 | convolution fusion | flops 859889664 | bytes 5568512 | tf_op jit(solution)/shard_map/anc,rdjn->dajrc/dot_general | solution.py:40
  32.5 0.0 copy-start.1
  32.5 0.9 fusion.53
  34.8 0.6 constant_dynamic-update-slice_fusion.15
  35.5 0.6 constant_dynamic-update-slice_fusion.14
  36.1 0.6 constant_dynamic-update-slice_fusion.13
  36.7 0.6 constant_dynamic-update-slice_fusion.12
  37.3 0.6 constant_dynamic-update-slice_fusion.11
  38.0 0.6 constant_dynamic-update-slice_fusion.10
  38.6 0.6 constant_dynamic-update-slice_fusion.9
  39.2 0.6 constant_dynamic-update-slice_fusion.8
  39.8 0.6 constant_dynamic-update-slice_fusion.7
  40.4 0.6 constant_dynamic-update-slice_fusion.6
  41.1 0.6 constant_dynamic-update-slice_fusion.5
  41.7 0.6 constant_dynamic-update-slice_fusion.4
  42.3 0.6 constant_dynamic-update-slice_fusion.3
  42.9 0.6 constant_dynamic-update-slice_fusion.2
  43.6 0.6 constant_dynamic-update-slice_fusion.1
  44.2 0.6 constant_dynamic-update-slice_fusion
  44.8 15.3 %all-to-all-start = ((bf16[16,1,6,6,512]{4,3,2,1,0:T(8,128)(2,1)}), bf16[16,1,6,6,512]{4,3,2,1,0:T(8,128)(2,1)S(1)}, u32[]{:S(2)}, u32[]{:S(2)}) async-start(bf16[16,1,6,6,512]{4,3,2,1,0:T(8,128)(2,1)} %constant_dynamic-update-slice_fusion), calls=%async_computation | async-start | bytes 1572864 | tf_op jit(solution)/shard_map/all_to_all | solution.py:45
  60.1 0.1 dynamic_slice.3
  60.2 0.1 iota_compare_fusion
  60.3 0.0 copy-done.1
  60.3 0.1 fusion.52
  60.3 1.2 %slice_bitcast_fusion = (bf16[6,256,256]{2,1,0:T(8,128)(2,1)}, bf16[6,256,256]{2,1,0:T(8,128)(2,1)}) fusion(bf16[6,2,256,256]{3,2,1,0:T(8,128)(2,1)S(1)} %copy-done.1), kind=kLoop, calls=%fused_computation.29 | loop fusion | bytes 3145728 | tf_op jit(solution)/shard_map/squeeze | solution.py:16
  61.6 18.2 %all-to-all-done = bf16[16,1,6,6,512]{4,3,2,1,0:T(8,128)(2,1)S(1)} async-done(((bf16[16,1,6,6,512]{4,3,2,1,0:T(8,128)(2,1)}), bf16[16,1,6,6,512]{4,3,2,1,0:T(8,128)(2,1)S(1)}, u32[]{:S(2)}, u32[]{:S(2)}) %all-to-all-start) | async-done | bytes 589856 | tf_op jit(solution)/shard_map/all_to_all | solution.py:45
  79.8 0.0 copy-done
  79.8 0.4 fusion.18
  80.1 2.4 %fusion.25 = bf16[96,6,512]{2,0,1:T(8,128)(2,1)S(1)} fusion(bf16[6,96,96]{2,1,0:T(8,128)(2,1)S(1)} %copy-done, bf16[6,512,96]{1,2,0:T(8,128)(2,1)S(1)} %fusion.18, bf16[6,256,256]{2,1,0:T(8,128)(2,1)} %get-tuple-element.10, bf16[6,256,256]{2,1,0:T(8,128)(2,1)S(1)} %fusion.52, bf16[6,256,256]{2,1,0:T(8,128)(2,1)} %get-tuple-element.9), kind=kOutput, calls=%fused_computation.25 | convolution fusion | flops 371785728 | bytes 3649536 | tf_op jit(solution)/shard_map/jlt,jld->tjd/dot_general | solution.py:63
  82.6 0.2 reshape.243
  82.8 1.0 copy.75
  83.7 4.4 %all-to-all-start.1 = ((bf16[16,6,6,512]{3,1,2,0:T(8,128)(2,1)}), bf16[16,6,6,512]{3,1,2,0:T(8,128)(2,1)S(1)}, u32[]{:S(2)}, u32[]{:S(2)}) async-start(bf16[16,6,6,512]{3,1,2,0:T(8,128)(2,1)} %copy.75), calls=%async_computation.1 | async-start | bytes 1572864 | tf_op jit(solution)/shard_map/all_to_all | solution.py:67
  88.2 2.9 %multiply_convert_fusion.1 = (bf16[1,96,1440]{2,1,0:T(8,128)(2,1)S(1)}, bf16[1,96,1440]{2,1,0:T(8,128)(2,1)S(1)}) fusion(s32[96]{0:T(128)S(1)} %copy-done.2, f32[96]{0:T(128)S(1)} %get-tuple-element.33, f32[96]{0:T(128)S(1)} %get-tuple-element.34), kind=kLoop, calls=%fused_computation.49 | loop fusion | flops 1797120 | bytes 554112 | tf_op jit(solution)/shard_map/convert.2
  91.0 16.7 %all-to-all-done.1 = bf16[16,6,6,512]{3,1,2,0:T(8,128)(2,1)S(1)} async-done(((bf16[16,6,6,512]{3,1,2,0:T(8,128)(2,1)}), bf16[16,6,6,512]{3,1,2,0:T(8,128)(2,1)S(1)}, u32[]{:S(2)}, u32[]{:S(2)}) %all-to-all-start.1) | async-done | bytes 589856 | tf_op jit(solution)/shard_map/all_to_all | solution.py:67
  107.8 0.3 reshape.248
  108.1 6.2 %fusion.3 = bf16[6,1440,256]{2,1,0:T(8,128)(2,1)} fusion(f32[256]{0:T(256)S(1)} %get-tuple-element.30, f32[256]{0:T(256)S(1)} %get-tuple-element.29, bf16[6,1440,256]{2,1,0:T(8,128)(2,1)} %param.5, bf16[1,96,1440]{2,1,0:T(8,128)(2,1)S(1)} %get-tuple-element.32, bf16[1,96,1440]{2,1,0:T(8,128)(2,1)S(1)} %get-tuple-element.31, ...), kind=kOutput, calls=%fused_computation.7 | convolution fusion | flops 868147200 | bytes 9992192 | tf_op jit(solution)/shard_map/akrc,rkn->anc/dot_general | solution.py:70
  (34 shorter events, 1.1 us)
Async XLA Ops:
  0.0 79.8 %copy-start = (bf16[6,96,96]{2,1,0:T(8,128)(2,1)S(1)}, bf16[6,96,96]{2,1,0:T(8,128)(2,1)}, u32[]{:S(2)}) copy-start(bf16[6,96,96]{2,1,0:T(8,128)(2,1)} %param.8) | copy-start | bytes 331780
  0.0 3.5 %copy-start.2 = (s32[96]{0:T(128)S(1)}, s32[96]{0:T(128)}, u32[]{:S(2)}) copy-start(s32[96]{0:T(128)} %param.7) | copy-start | bytes 1156
  0.0 28.8 %copy-start.3 = (f32[256]{0:T(256)S(1)}, f32[256]{0:T(256)}, u32[]{:S(2)}) copy-start(f32[256]{0:T(256)} %param.6) | copy-start | bytes 3076
  32.5 27.8 %copy-start.1 = (bf16[6,2,256,256]{3,2,1,0:T(8,128)(2,1)S(1)}, bf16[6,2,256,256]{3,2,1,0:T(8,128)(2,1)}, u32[]{:S(2)}) copy-start(bf16[6,2,256,256]{3,2,1,0:T(8,128)(2,1)} %param.9) | copy-start | bytes 4718596
  44.8 34.9 %all-to-all-start = ((bf16[16,1,6,6,512]{4,3,2,1,0:T(8,128)(2,1)}), bf16[16,1,6,6,512]{4,3,2,1,0:T(8,128)(2,1)S(1)}, u32[]{:S(2)}, u32[]{:S(2)}) async-start(bf16[16,1,6,6,512]{4,3,2,1,0:T(8,128)(2,1)} %constant_dynamic-update-slice_fusion), calls=%async_computation | async-start | bytes 1572864 | tf_op jit(solution)/shard_map/all_to_all | solution.py:45
  83.7 24.0 %all-to-all-start.1 = ((bf16[16,6,6,512]{3,1,2,0:T(8,128)(2,1)}), bf16[16,6,6,512]{3,1,2,0:T(8,128)(2,1)S(1)}, u32[]{:S(2)}, u32[]{:S(2)}) async-start(bf16[16,6,6,512]{3,1,2,0:T(8,128)(2,1)} %copy.75), calls=%async_computation.1 | async-start | bytes 1572864 | tf_op jit(solution)/shard_map/all_to_all | solution.py:67
